TPU v7x, 32 devices: a whole 2x2x4 slice. The times are simulated.
32 devices in a mesh: inter: 16 (over z, y, core), intra: 2 (over x).
Axes of the slice: x: 2, y: 2, z: 4, core: 2. Of those that a mesh axis runs over, the one named last changes fastest.
Arguments:
- hidden_in: bfloat16 [16, 256, 4096], P('inter', 'intra'), may hold values from -120 to 120, as said below
- norm_gain: bfloat16 [4096], P(('inter', 'intra')), may hold values from 0.5 to 2, as said below
- qkv_weight: bfloat16 [4096, 768], P(('inter', 'intra')), may hold values from -0.09375 to 0.09375
- attn_cotangent: bfloat16 [16, 256, 512], P('inter', 'intra'), may hold values from -6 to 6
Outputs:
- attn: bfloat16 [16, 256, 512], P('inter', 'intra')
- grad_in: bfloat16 [16, 256, 4096], P('inter', 'intra')
- weight_grad: float32 [4096, 768], P(('intra', 'inter'))
- gain_grad: float32 [4096], P(('intra', 'inter'))
Inputs may be any that keep to these rules, and one draw needn't show every extreme that they name: `hidden_in`: activations with spread row and feature scales. `norm_gain`: positive gains.
All inputs are finite; a program needn't handle non-finite values.
Results may differ from a plain program's by a relative error of at most 0.015.
Values may be sent and summed in bfloat16 or wider, within the bound.
No kernel may reach another device: no remote copies, remote signals or barrier semaphores. Data moves between devices by JAX's collectives and lax.ppermute only.
A program may use at most 64 MiB of HBM per device.

v0:
```python
import jax
import jax.numpy as jnp
from jax import lax
from jax.sharding import PartitionSpec as P

HD = 128
HEADS = 4


eps_norm = 1e-05
rope_base = 500000.0


def rope_tables(positions, head_size):
    half_size = head_size // 2
    freqs = rope_base ** (-jnp.arange(half_size, dtype=jnp.float32) / half_size)
    angles = positions.astype(jnp.float32)[:, None] * freqs[None, :]
    return (jnp.cos(angles), jnp.sin(angles))


def rotate(values_in, cosine, sine):
    half_size = values_in.shape[-1] // 2
    first, second = (values_in[..., :half_size], values_in[..., half_size:])
    return jnp.concatenate(
        [first * cosine - second * sine, second * cosine + first * sine], axis=-1
    )


def unrotate(grad_out, cosine, sine):
    half_size = grad_out.shape[-1] // 2
    first, second = (grad_out[..., :half_size], grad_out[..., half_size:])
    return jnp.concatenate(
        [first * cosine + second * sine, second * cosine - first * sine], axis=-1
    )


def forward_fold(query_rows, row_pos):

    def forward_advance(carry, piece, start):
        row_top, row_total, weighted = carry
        key_part, value_part = piece
        scores = jnp.einsum("qd,kd->qk", query_rows, key_part, preferred_element_type=jnp.float32)
        key_pos = jnp.arange(key_part.shape[0], dtype=jnp.int32)
        allowed = key_pos[None, :] <= row_pos[:, None]
        scores = jnp.where(allowed, scores, -1e30)
        new_top = jnp.maximum(row_top, jnp.max(scores, axis=1))
        numbers = jnp.where(allowed, jnp.exp(scores - new_top[:, None]), 0.0)
        row_total = jnp.sum(numbers, axis=1)
        weighted = jnp.dot(
            numbers,
            value_part.astype(jnp.float32),
            precision=lax.Precision.HIGHEST,
            preferred_element_type=jnp.float32,
        )
        return (new_top, row_total, weighted)

    return forward_advance


def query_grad_fold(query_rows, row_pos, grad_flat, log_total, row_delta):

    def query_advance(grad_query, piece, start):
        key_part, value_part = piece
        scores = jnp.einsum("qd,kd->qk", query_rows, key_part, preferred_element_type=jnp.float32)
        key_pos = jnp.arange(key_part.shape[0], dtype=jnp.int32)
        allowed = key_pos[None, :] <= row_pos[:, None]
        probs = jnp.where(
            allowed, jnp.exp(jnp.where(allowed, scores, -1e30) - log_total[:, None]), 0.0
        )
        grad_probs = jnp.einsum(
            "qd,kd->qk", grad_flat, value_part, preferred_element_type=jnp.float32
        )
        grad_scores = (probs * (grad_probs - row_delta[:, None])).astype(jnp.bfloat16)
        return jnp.dot(grad_scores, key_part, preferred_element_type=jnp.float32)

    return query_advance


def key_grad_fold(key_rows, value_rows, key_pos, log_all, delta_all, heads_count):

    def key_advance(carry, piece, start):
        query_part, attn_grad_part = piece
        count = query_part.shape[0]
        scores = jnp.einsum("qd,kd->qk", query_part, key_rows, preferred_element_type=jnp.float32)
        query_pos = jnp.arange(count, dtype=jnp.int32) // heads_count
        allowed = key_pos[None, :] <= query_pos[:, None]
        probs = jnp.where(
            allowed, jnp.exp(jnp.where(allowed, scores, -1e30) - log_all[:, None]), 0.0
        )
        grad_values = jnp.einsum(
            "qk,qd->kd",
            probs.astype(jnp.bfloat16),
            attn_grad_part,
            preferred_element_type=jnp.float32,
        )
        grad_probs = jnp.einsum(
            "qd,kd->qk", attn_grad_part, value_rows, preferred_element_type=jnp.float32
        )
        grad_scores = (probs * (grad_probs - delta_all[:, None])).astype(jnp.bfloat16)
        grad_keys = jnp.einsum(
            "qk,qd->kd", grad_scores, query_part, preferred_element_type=jnp.float32
        )
        return (grad_keys, grad_values)

    return key_advance


def local(hidden_in, norm_gain, qkv_weight, attn_cotangent):
    rows_in = hidden_in[0]
    grad_attn = attn_cotangent[0]
    tokens_here = rows_in.shape[0]
    width = rows_in.shape[1]
    head_size = HD
    heads_count = HEADS
    qcols = heads_count * head_size
    scale = head_size ** (-0.5)
    weight_group, gain_group = (
        lax.all_gather(qkv_weight, "intra", axis=0, tiled=True),
        lax.all_gather(norm_gain, "intra", axis=0, tiled=True),
    )
    weight_full, gain_full = (
        lax.all_gather(weight_group, "inter", axis=0, tiled=True),
        lax.all_gather(gain_group, "inter", axis=0, tiled=True),
    )
    query_pos = lax.axis_index("intra") * tokens_here + jnp.arange(tokens_here, dtype=jnp.int32)
    row_pos = jnp.broadcast_to(query_pos[:, None], (tokens_here, heads_count)).reshape(
        tokens_here * heads_count
    )
    cosine, sine = rope_tables(query_pos, head_size)
    wide_rows = rows_in.astype(jnp.float32)
    inv_rms = lax.rsqrt(jnp.mean(wide_rows * wide_rows, axis=1, keepdims=True) + eps_norm)
    normed = (wide_rows * inv_rms * gain_full.astype(jnp.float32)[None, :]).astype(jnp.bfloat16)
    mixed = jnp.dot(normed, weight_full, preferred_element_type=jnp.float32)
    query_rows = (
        (
            rotate(
                mixed[:, :qcols].reshape(tokens_here, heads_count, head_size),
                cosine[:, None, :],
                sine[:, None, :],
            )
            * scale
        )
        .astype(jnp.bfloat16)
        .reshape(tokens_here * heads_count, head_size)
    )
    key_rows = rotate(mixed[:, qcols : qcols + head_size], cosine, sine).astype(jnp.bfloat16)
    value_rows = mixed[:, qcols + head_size :].astype(jnp.bfloat16)
    grad_flat = grad_attn.reshape(tokens_here * heads_count, head_size)
    flat_rows = tokens_here * heads_count
    forward_step = forward_fold(query_rows, row_pos)
    start_carry = (
        jnp.full((flat_rows,), -1e30, jnp.float32),
        jnp.zeros((flat_rows,), jnp.float32),
        jnp.zeros((flat_rows, head_size), jnp.float32),
    )
    row_top, row_total, weighted = forward_step(
        start_carry,
        (
            lax.all_gather(key_rows, "intra", axis=0, tiled=True),
            lax.all_gather(value_rows, "intra", axis=0, tiled=True),
        ),
        jnp.int32(0),
    )
    attn_flat = (weighted / row_total[:, None]).astype(jnp.bfloat16)
    log_total = row_top + jnp.log(row_total)
    row_delta = jnp.sum(grad_flat.astype(jnp.float32) * attn_flat.astype(jnp.float32), axis=1)
    query_step = query_grad_fold(query_rows, row_pos, grad_flat, log_total, row_delta)
    grad_query = query_step(
        jnp.zeros((flat_rows, head_size), jnp.float32),
        (
            lax.all_gather(key_rows, "intra", axis=0, tiled=True),
            lax.all_gather(value_rows, "intra", axis=0, tiled=True),
        ),
        jnp.int32(0),
    )
    log_all, delta_all = (
        lax.all_gather(log_total, "intra", axis=0, tiled=True),
        lax.all_gather(row_delta, "intra", axis=0, tiled=True),
    )
    key_step = key_grad_fold(key_rows, value_rows, query_pos, log_all, delta_all, heads_count)
    grad_keys, grad_values = key_step(
        (
            jnp.zeros((tokens_here, head_size), jnp.float32),
            jnp.zeros((tokens_here, head_size), jnp.float32),
        ),
        (
            lax.all_gather(query_rows, "intra", axis=0, tiled=True),
            lax.all_gather(grad_flat, "intra", axis=0, tiled=True),
        ),
        jnp.int32(0),
    )
    query_back = (
        unrotate(
            grad_query.reshape(tokens_here, heads_count, head_size),
            cosine[:, None, :],
            sine[:, None, :],
        )
        * scale
    ).reshape(tokens_here, qcols)
    grad_mixed = jnp.concatenate(
        [query_back, unrotate(grad_keys, cosine, sine), grad_values], axis=1
    ).astype(jnp.bfloat16)
    weight_back, gain_back = (weight_full, gain_full)
    gain_wide = gain_back.astype(jnp.float32)[None, :]
    grad_normed = jnp.einsum(
        "tc,dc->td", grad_mixed, weight_back, preferred_element_type=jnp.float32
    )
    inner = jnp.sum(grad_normed * gain_wide * wide_rows, axis=1, keepdims=True)
    grad_rows = (
        gain_wide * grad_normed * inv_rms - wide_rows * inv_rms**3 / width * inner
    ).astype(jnp.bfloat16)
    gain_term = jnp.sum(grad_normed * wide_rows * inv_rms, axis=0)
    normed_cols = lax.all_to_all(normed, "intra", split_axis=1, concat_axis=0, tiled=True)
    group_term = lax.dot_general(
        normed_cols,
        lax.all_gather(grad_mixed, "intra", axis=0, tiled=True),
        (((0,), (0,)), ((), ())),
        preferred_element_type=jnp.float32,
    )
    term_low = lax.optimization_barrier(group_term.astype(jnp.bfloat16))
    gain_sums = lax.psum_scatter(gain_term, "intra", scatter_dimension=0, tiled=True)
    weight_grad, gain_grad = (
        lax.psum_scatter(term_low.astype(jnp.float32), "inter", scatter_dimension=0, tiled=True),
        lax.psum_scatter(gain_sums, "inter", scatter_dimension=0, tiled=True),
    )
    return (attn_flat.reshape(tokens_here, qcols)[None], grad_rows[None], weight_grad, gain_grad)


def solution(mesh):
    return jax.shard_map(
        local,
        mesh=mesh,
        in_specs=(
            P("inter", "intra", None),
            P(("inter", "intra")),
            P(("inter", "intra"), None),
            P("inter", "intra", None),
        ),
        out_specs=(
            P("inter", "intra", None),
            P("inter", "intra", None),
            P(("intra", "inter"), None),
            P(("intra", "inter")),
        ),
        check_vma=False,
    )
```

profile of v0, /device:TPU:0, one launch (start us, length us, event | category | flops | bytes accessed | tf_op | source)
XLA Modules:
  0.0 226.0 jit_solution(16348973796730813861)
XLA Ops:
  7.2 10.6 %all_gather.37 = bf16[256,768]{1,0:T(8,128)(2,1)} all-gather(bf16[128,768]{1,0:T(8,128)(2,1)} %param.6), channel_id=1, replica_groups=mesh['inter'=16,'intra'=2] {'intra'}, dimensions={0}, use_global_device_ids=true | all-gather | bytes 589824 | tf_op jit(solution)/shard_map/all_gather | solution.py:118
  17.8 4.4 %all-gather = bf16[2,1,128]{2,1,0:T(2,128)(2,1)S(1)} all-gather(bf16[1,1,128]{2,1,0:T(2,128)(2,1)} %bitcast.94), channel_id=1, replica_groups=mesh['inter'=16,'intra'=2] {'intra'}, dimensions={0}, use_global_device_ids=true | all-gather | bytes 768 | tf_op jit(solution)/shard_map/all_gather | solution.py:119
  22.2 22.1 %all-gather.1 = bf16[16,1,256]{2,1,0:T(2,128)(2,1)S(1)} all-gather(bf16[1,1,256]{2,1,0:T(2,128)(2,1)S(1)} %bitcast.93), channel_id=1, replica_groups=mesh['inter'=16,'intra'=2] {'inter'}, dimensions={0}, use_global_device_ids=true | all-gather | bytes 8704 | tf_op jit(solution)/shard_map/all_gather | solution.py:123
  44.3 3.1 %reshape.149 = f32[128,2,2048]{2,1,0:T(2,128)S(1)} reshape(bf16[1,128,4096]{2,1,0:T(8,128)(2,1)} %param.4) | data formatting | bytes 3145728 | tf_op jit(solution)/shard_map/convert_element_type | solution.py:130
  48.4 2.1 fusion.10
  50.5 3.6 %all-to-all-start = ((bf16[128,2,2048]{2,0,1:T(8,128)(2,1)}), bf16[128,2,2048]{2,0,1:T(8,128)(2,1)S(1)}, u32[]{:S(2)}, u32[]{:S(2)}) async-start(bf16[128,2,2048]{2,0,1:T(8,128)(2,1)} %fusion.10), calls=%async_computation | async-start | bytes 2097152 | tf_op jit(solution)/shard_map/all_to_all | solution.py:213
  55.9 15.4 %all_gather.43 = bf16[1024,128]{1,0:T(8,128)(2,1)S(1)} all-gather(bf16[512,128]{1,0:T(8,128)(2,1)S(1)} %reshape_squeeze.3), channel_id=1, replica_groups=mesh['inter'=16,'intra'=2] {'intra'}, dimensions={0}, use_global_device_ids=true | all-gather | bytes 393216 | tf_op jit(solution)/shard_map/all_gather | solution.py:188
  71.9 7.8 %all-gather.6.cloned.1.call-done = bf16[4096,768]{1,0:T(8,128)(2,1)} async-done(((bf16[256,768]{1,0:T(8,128)(2,1)}), bf16[4096,768]{1,0:T(8,128)(2,1)}) %all-gather.6.cloned.1.call-update) | async-done | bytes 6291472 | tf_op jit(solution)/shard_map/all_gather | solution.py:122
  79.7 3.8 %fusion.24 = f32[128,768]{1,0:T(8,128)S(1)} fusion(bf16[4096,768]{1,0:T(8,128)(2,1)} %all-gather.6.cloned.1.call-done, bf16[1,128,4096]{2,1,0:T(8,128)(2,1)S(1)} %copy-done, f32[4096]{0:T(1024)S(1)} %bitcast.86, f32[128]{0:T(128)} %copy-done.11), kind=kOutput, calls=%fused_computation.37 | convolution fusion | flops 807403520 | bytes 7750144 | tf_op jit(solution)/shard_map/dot_general | solution.py:133
  83.6 4.7 %all_gather.40 = bf16[256,128]{1,0:T(8,128)(2,1)} all-gather(bf16[128,128]{1,0:T(8,128)(2,1)S(1)} %slice.71), channel_id=1, replica_groups=mesh['inter'=16,'intra'=2] {'intra'}, dimensions={0}, use_global_device_ids=true | all-gather | bytes 98304 | tf_op jit(solution)/shard_map/all_gather | solution.py:160
  89.4 4.7 %all_gather.39 = bf16[256,128]{1,0:T(8,128)(2,1)} all-gather(bf16[128,128]{1,0:T(8,128)(2,1)S(1)} %pad_maximum_fusion.1), channel_id=1, replica_groups=mesh['inter'=16,'intra'=2] {'intra'}, dimensions={0}, use_global_device_ids=true | all-gather | bytes 98304 | tf_op jit(solution)/shard_map/all_gather | solution.py:159
  94.6 5.7 %all_gather.41 = bf16[1024,128]{1,0:T(8,128)(2,1)} all-gather(bf16[512,128]{1,0:T(8,128)(2,1)S(1)} %fusion.32), channel_id=1, replica_groups=mesh['inter'=16,'intra'=2] {'intra'}, dimensions={0}, use_global_device_ids=true | all-gather | bytes 393216 | tf_op jit(solution)/shard_map/all_gather | solution.py:187
  103.1 2.1 fusion.20
  105.2 4.7 %all-gather.2 = f32[2,1,512]{2,1,0:T(1,128)S(1)} all-gather(f32[1,1,512]{2,1,0:T(1,128)} %bitcast.90), channel_id=1, replica_groups=mesh['inter'=16,'intra'=2] {'intra'}, dimensions={0}, use_global_device_ids=true | all-gather | bytes 6144 | tf_op jit(solution)/shard_map/all_gather | solution.py:177
  109.9 5.3 %all-gather.3 = f32[2,1,512]{2,1,0:T(1,128)} all-gather(f32[1,1,512]{2,1,0:T(1,128)} %bitcast.92), channel_id=1, replica_groups=mesh['inter'=16,'intra'=2] {'intra'}, dimensions={0}, use_global_device_ids=true | all-gather | bytes 6144 | tf_op jit(solution)/shard_map/all_gather | solution.py:178
  115.2 2.0 multiply_add_fusion
  119.5 1.8 fusion.21
  124.8 6.3 %all_gather.45 = bf16[256,768]{1,0:T(8,128)(2,1)S(1)} all-gather(bf16[128,768]{1,0:T(8,128)(2,1)S(1)} %pad_maximum_fusion), channel_id=1, replica_groups=mesh['inter'=16,'intra'=2] {'intra'}, dimensions={0}, use_global_device_ids=true | all-gather | bytes 589824 | tf_op jit(solution)/shard_map/all_gather | solution.py:216
  132.2 3.1 %convert_element_type.81 = f32[2048,768]{1,0:T(8,128)} convert(bf16[2048,768]{1,0:T(8,128)(2,1)S(1)} %convolution_convert_fusion) | non-fusion elementwise | flops 1572864 | bytes 9437184 | tf_op jit(solution)/shard_map/convert_element_type | solution.py:223
  139.3 5.6 %fusion.8 = (f32[4096]{0:T(1024)S(1)}, f32[128]{0:T(128)S(1)}, f32[128,4096]{1,0:T(8,128)S(1)}) fusion(bf16[1,128,4096]{2,1,0:T(8,128)(2,1)S(1)} %copy-done, f32[128]{0:T(128)S(1)} %copy-done.12, f32[4096]{0:T(1024)S(1)} %bitcast.87, bf16[128,768]{1,0:T(8,128)(2,1)S(1)} %pad_maximum_fusion, bf16[4096,768]{1,0:T(8,128)(2,1)} %all-gather.6.cloned.1.call-done), kind=kOutput, calls=%fused_computation.14 | convolution fusion | flops 808972160 | bytes 9667584 | tf_op jit(solution)/shard_map/tc,dc->td/dot_general | solution.py:205
  144.9 7.1 %all-reduce = f32[4096]{0:T(1024)S(1)} all-reduce(f32[4096]{0:T(1024)S(1)} %get-tuple-element.4), channel_id=3, replica_groups=mesh['inter'=16,'intra'=2] {'intra'}, use_global_device_ids=true, to_apply=%region_7.8.clone | all-reduce | flops 4096 | bytes 32768
  152.1 30.9 %all-reduce.1 = f32[2048]{0:T(1024)S(1)} all-reduce(f32[2048]{0:T(1024)S(1)} %dynamic-slice.1), channel_id=4, replica_groups=mesh['inter'=16,'intra'=2] {'inter'}, use_global_device_ids=true, to_apply=%region_8.9.clone | all-reduce | flops 2048 | bytes 16384
  183.6 1.6 fusion.23
  185.2 34.0 %reduce-scatter.2.cloned.1.call-done = f32[128,768]{1,0:T(8,128)} async-done(((f32[2048,768]{1,0:T(8,128)}), f32[128,768]{1,0:T(8,128)}) %reduce-scatter.2.cloned.1.call-update) | async-done | bytes 393232 | tf_op jit(solution)/shard_map/reduce_scatter | solution.py:223
  (85 shorter events, 17.6 us)
Async XLA Ops:
  7.2 40.3 %copy-start = (bf16[1,128,4096]{2,1,0:T(8,128)(2,1)S(1)}, bf16[1,128,4096]{2,1,0:T(8,128)(2,1)}, u32[]{:S(2)}) copy-start(bf16[1,128,4096]{2,1,0:T(8,128)(2,1)} %param.4) | copy-start | bytes 3145732
  7.2 72.5 %all-gather.6.cloned.1.call-start = ((), (), s32[]{:S(2)}) async-start(), calls=%async_computation.2 | async-start | bytes 6684672 | tf_op jit(solution)/shard_map/all_gather | solution.py:122
  48.4 2.1 copy-start.11
  48.4 6.6 %copy-start.6 = (bf16[1,128,512]{2,1,0:T(8,128)(2,1)S(1)}, bf16[1,128,512]{2,1,0:T(8,128)(2,1)}, u32[]{:S(2)}) copy-start(bf16[1,128,512]{2,1,0:T(8,128)(2,1)} %param.7) | copy-start | bytes 393220
  50.5 80.6 %all-to-all-start = ((bf16[128,2,2048]{2,0,1:T(8,128)(2,1)}), bf16[128,2,2048]{2,0,1:T(8,128)(2,1)S(1)}, u32[]{:S(2)}, u32[]{:S(2)}) async-start(bf16[128,2,2048]{2,0,1:T(8,128)(2,1)} %fusion.10), calls=%async_computation | async-start | bytes 2097152 | tf_op jit(solution)/shard_map/all_to_all | solution.py:213
  54.1 165.0 %reduce-scatter.2.cloned.1.call-start = ((), (), s32[]{:S(2)}) async-start(), calls=%async_computation.3 | async-start | bytes 6684672 | tf_op jit(solution)/shard_map/reduce_scatter | solution.py:223
  54.2 0.9 copy-start.17
  71.3 17.0 %copy-start.13 = (f32[128]{0:T(128)}, f32[128]{0:T(128)S(1)}, u32[]{:S(2)}) copy-start(f32[128]{0:T(128)S(1)} %fusion.64) | copy-start | bytes 1540
  71.3 17.0 %copy-start.14 = (f32[64]{0:T(128)}, f32[64]{0:T(128)S(1)}, u32[]{:S(2)}) copy-start(f32[64]{0:T(128)S(1)} %multiply_power_fusion) | copy-start | bytes 772
  88.6 12.1 %copy-start.2 = (f32[128,64]{1,0:T(8,128)}, f32[128,64]{1,0:T(8,128)S(1)}, u32[]{:S(2)}) copy-start(f32[128,64]{1,0:T(8,128)S(1)} %get-tuple-element.14) | copy-start | bytes 98308
  88.6 12.1 %copy-start.3 = (f32[128,64]{1,0:T(8,128)}, f32[128,64]{1,0:T(8,128)S(1)}, u32[]{:S(2)}) copy-start(f32[128,64]{1,0:T(8,128)S(1)} %get-tuple-element.15) | copy-start | bytes 98308
  88.7 0.6 copy-start.5
  94.1 6.2 %copy-start.4 = (bf16[256,128]{1,0:T(8,128)(2,1)S(1)}, bf16[256,128]{1,0:T(8,128)(2,1)}, u32[]{:S(2)}) copy-start(bf16[256,128]{1,0:T(8,128)(2,1)} %all_gather.39) | copy-start | bytes 196612
  94.1 6.2 %copy-start.10 = (s32[512]{0:T(512)S(1)}, s32[512]{0:T(512)}, u32[]{:S(2)}) copy-start(s32[512]{0:T(512)} %le.15) | copy-start | bytes 6148
  94.1 7.2 %copy-start.8 = (bf16[512,128]{0,1:T(8,128)(2,1)S(1)}, bf16[512,128]{0,1:T(8,128)(2,1)}, u32[]{:S(2)}) copy-start(bf16[512,128]{0,1:T(8,128)(2,1)} %copy.18) | copy-start | bytes 393220
  94.2 7.2 %copy-start.9 = (bf16[256,128]{1,0:T(8,128)(2,1)S(1)}, bf16[256,128]{1,0:T(8,128)(2,1)}, u32[]{:S(2)}) copy-start(bf16[256,128]{1,0:T(8,128)(2,1)} %all_gather.40) | copy-start | bytes 196612
  102.5 0.6 copy-start.15
  105.2 14.3 %copy-start.1 = (bf16[1024,128]{1,0:T(8,128)(2,1)S(1)}, bf16[1024,128]{1,0:T(8,128)(2,1)}, u32[]{:S(2)}) copy-start(bf16[1024,128]{1,0:T(8,128)(2,1)} %all_gather.41) | copy-start | bytes 786436
  135.3 0.7 copy-start.19
  135.3 1.3 copy-start.18
  135.3 3.1 %copy-start.7 = (bf16[512,128]{0,1:T(8,128)(2,1)S(1)}, bf16[512,128]{0,1:T(8,128)(2,1)}, u32[]{:S(2)}) copy-start(bf16[512,128]{0,1:T(8,128)(2,1)} %get-tuple-element.21) | copy-start | bytes 393220
  135.3 4.0 %copy-start.12 = (f32[128]{0:T(128)S(1)}, f32[128]{0:T(128)}, u32[]{:S(2)}) copy-start(f32[128]{0:T(128)} %copy-done.11) | copy-start | bytes 1540
  139.3 44.3 %copy-start.16 = (f32[128]{0:T(128)S(1)}, f32[128]{0:T(128)}, u32[]{:S(2)}) copy-start(f32[128]{0:T(128)} %get-tuple-element.16) | copy-start | bytes 1540
Sparse Core Ops, SparseCore 0:
  17.9 61.7 all-gather.5
  135.4 83.6 reduce-scatter.1
where the time goes:
time: 227 us; the launch traced here: 226 us
  blocking collectives  122 us (54%)
  waiting for transfers between devices  41.8 us (18%)
  matrix products  18 us (8%)
  between operations  15.7 us (7%)
  other arithmetic  14.6 us (6%)
  local copies, waits for them, and re-layouts  10.3 us (5%)
  starting transfers between devices  3.67 us (2%)
    unnamed x2, blocking collectives  38.1 us
    reduce_scatter x1, waiting for transfers between devices, local(): lax.psum_scatter(term_low.astype(jnp.float32), 'inter', scatter_dimension...  34 us
    all_gather x1, blocking collectives, local(): lax.all_gather(gain_group, 'inter', axis=0, tiled=True)  22.1 us
    all_gather x1, blocking collectives, local(): lax.all_gather(grad_flat, 'intra', axis=0, tiled=True)  15.4 us
    all_gather x1, blocking collectives, local(): lax.all_gather(qkv_weight, 'intra', axis=0, tiled=True)  10.6 us
    all_gather x1, waiting for transfers between devices, local(): lax.all_gather(weight_group, 'inter', axis=0, tiled=True)  7.82 us
    all_gather x1, blocking collectives, local(): lax.all_gather(grad_mixed, 'intra', axis=0, tiled=True)  6.34 us
    all_gather x1, blocking collectives, local(): lax.all_gather(query_rows, 'intra', axis=0, tiled=True)  5.74 us
  transfers between devices with their start and end apart: 3, of which 2 were waited for; matrix products, arithmetic and copies ran while one was open for 16% of the time, Pallas kernels for 0%

commit v1 on v0

--- a/solution.py
+++ b/solution.py
@@ -1,6 +1,8 @@
 import jax
 import jax.numpy as jnp
 from jax import lax
+from jax.experimental import pallas as pl
+from jax.experimental.pallas import tpu as pltpu
 from jax.sharding import PartitionSpec as P
 
 HD = 128
@@ -105,7 +107,7 @@
     return key_advance
 
 
-def local(hidden_in, norm_gain, qkv_weight, attn_cotangent):
+def generic_local(hidden_in, norm_gain, qkv_weight, attn_cotangent):
     rows_in = hidden_in[0]
     grad_attn = attn_cotangent[0]
     tokens_here = rows_in.shape[0]
@@ -226,7 +228,341 @@
     return (attn_flat.reshape(tokens_here, qcols)[None], grad_rows[None], weight_grad, gain_grad)
 
 
+LANES = 128
+NEG = -1e30
+
+
+def partial_kernel(slots, own_ref, peer_ref, *rest):
+    pieces, (out_ref, rows, sems) = rest[:-3], rest[-3:]
+    block = pieces[0].shape[0]
+    copies = [
+        pltpu.make_async_copy(
+            piece, rows.at[pl.ds(pl.multiple_of(slots[n] * block, block), block)], sems.at[n]
+        )
+        for n, piece in enumerate(pieces)
+    ]
+    for copy in copies:
+        copy.start()
+    for copy in copies:
+        copy.wait()
+    tokens = own_ref.shape[0]
+    out_ref[:tokens] = jnp.dot(
+        own_ref[...], rows[...], preferred_element_type=jnp.float32
+    ).astype(jnp.bfloat16)
+    out_ref[tokens:] = jnp.dot(
+        peer_ref[...], rows[...], preferred_element_type=jnp.float32
+    ).astype(jnp.bfloat16)
+
+
+def back_kernel(slots, grads_ref, *rest):
+    pieces, (own_ref, peer_ref, rows, sems) = rest[:-4], rest[-4:]
+    block = pieces[0].shape[0]
+    copies = [
+        pltpu.make_async_copy(
+            piece, rows.at[pl.ds(pl.multiple_of(slots[n] * block, block), block)], sems.at[n]
+        )
+        for n, piece in enumerate(pieces)
+    ]
+    for copy in copies:
+        copy.start()
+    for copy in copies:
+        copy.wait()
+    tokens = own_ref.shape[0]
+    dims = (((1,), (1,)), ((), ()))
+    peer_ref[...] = lax.dot_general(
+        grads_ref[tokens:], rows[...], dims, preferred_element_type=jnp.float32
+    ).astype(jnp.bfloat16)
+    own_ref[...] = lax.dot_general(
+        grads_ref[:tokens], rows[...], dims, preferred_element_type=jnp.float32
+    )
+
+
+def split_kernel(where, x_ref, own_ref, send_ref, own_half, send_half, rms_ref):
+    j = where[0]
+    tokens, width = x_ref.shape
+    half = width // 2
+    square = jnp.zeros((tokens, LANES), jnp.float32)
+    for n in range(half // LANES):
+        for part, out in ((j, own_ref), (1 - j, send_ref)):
+            start = pl.multiple_of((2 * n + part) * LANES, LANES)
+            piece = x_ref[:, pl.ds(start, LANES)]
+            out[:, n * LANES : (n + 1) * LANES] = piece
+            wide = piece.astype(jnp.float32)
+            square = square + wide * wide
+    own_half[...] = x_ref[:, pl.ds(pl.multiple_of(j * half, LANES), half)]
+    send_half[...] = x_ref[:, pl.ds(pl.multiple_of((1 - j) * half, LANES), half)]
+    total = jnp.sum(square, axis=1, keepdims=True)
+    rms_ref[...] = jnp.broadcast_to(lax.rsqrt(total / width + eps_norm), (tokens, LANES))
+
+
+def attention_kernel(
+    where, part_ref, peer_ref, rms_own, rms_peer, cot_own, cot_peer, cos_ref, sin_ref,
+    attn_ref, grads_ref, pull_ref, *, width,
+):
+    j = where[0]
+    tokens = rms_own.shape[0]
+    total = 2 * tokens
+    qcols = HEADS * HD
+    scale = HD ** (-0.5)
+    swap = peer_ref[...].astype(jnp.float32)
+    raw = part_ref[...].astype(jnp.float32) + jnp.concatenate([swap[tokens:], swap[:tokens]], axis=0)
+    rms = jnp.concatenate([rms_own[...], rms_peer[...]], axis=0)
+    rms_col = rms[:, :1]
+    mixed = raw * rms_col
+    cosine, sine = cos_ref[...], sin_ref[...]
+
+    def turn(u):
+        return u * cosine + pltpu.roll(u, HD // 2, 1) * sine
+
+    def unturn(u):
+        return u * cosine - pltpu.roll(u, HD // 2, 1) * sine
+
+    def position(axis):
+        index = lax.broadcasted_iota(jnp.int32, (total, total), axis)
+        return jnp.where(index < tokens, index + j * tokens, index - j * tokens)
+
+    allowed = position(1) <= position(0)
+    keys = turn(mixed[:, qcols : qcols + HD]).astype(jnp.bfloat16)
+    values = mixed[:, qcols + HD :].astype(jnp.bfloat16)
+    grad_keys = jnp.zeros((total, HD), jnp.float32)
+    grad_values = jnp.zeros((total, HD), jnp.float32)
+    inner = jnp.zeros((total, HD), jnp.float32)
+    rows_rows = (((1,), (1,)), ((), ()))
+    cols_cols = (((0,), (0,)), ((), ()))
+
+    def dot(a, b, dims):
+        return lax.dot_general(a, b, dims, preferred_element_type=jnp.float32)
+
+    for h in range(HEADS):
+        span = slice(h * HD, (h + 1) * HD)
+        query = (turn(mixed[:, span]) * scale).astype(jnp.bfloat16)
+        cot = jnp.concatenate([cot_own[:, span], cot_peer[:, span]], axis=0)
+        scores = jnp.where(allowed, dot(query, keys, rows_rows), NEG)
+        top = jnp.max(scores, axis=1, keepdims=True)
+        numbers = jnp.exp(scores - top)
+        share = 1.0 / jnp.sum(numbers, axis=1, keepdims=True)
+        probs = numbers * share
+        probs_low = probs.astype(jnp.bfloat16)
+        grad_probs = dot(cot, values, rows_rows)
+        delta = jnp.sum(probs * grad_probs, axis=1, keepdims=True)
+        grad_scores = (probs * (grad_probs - delta)).astype(jnp.bfloat16)
+        attn_ref[:, span] = (
+            jnp.dot(
+                numbers[:tokens].astype(jnp.bfloat16), values, preferred_element_type=jnp.float32
+            )
+            * share[:tokens]
+        ).astype(jnp.bfloat16)
+        grad_query = unturn(jnp.dot(grad_scores, keys, preferred_element_type=jnp.float32)) * scale
+        grads_ref[:, span] = (grad_query * rms_col).astype(jnp.bfloat16)
+        inner = inner + grad_query * mixed[:, span]
+        grad_keys = grad_keys + dot(grad_scores, query, cols_cols)
+        grad_values = grad_values + dot(probs_low, cot, cols_cols)
+    grad_keys = unturn(grad_keys)
+    inner = inner + grad_keys * mixed[:, qcols : qcols + HD] + grad_values * mixed[:, qcols + HD :]
+    grads_ref[:, qcols : qcols + HD] = (grad_keys * rms_col).astype(jnp.bfloat16)
+    grads_ref[:, qcols + HD :] = (grad_values * rms_col).astype(jnp.bfloat16)
+    pull = jnp.sum(inner[:tokens], axis=1, keepdims=True) * (1.0 / width)
+    pull_ref[...] = pull * rms_own[...] * rms_own[...]
+
+
+def term_kernel(slots, grads_ref, next_ref, a_ref, b_ref, c_ref, d_ref, *outs):
+    tokens = a_ref.shape[0]
+    dims = (((0,), (0,)), ((), ()))
+    for n, out in enumerate(outs):
+        block = out.shape[0]
+        span = pl.ds(pl.multiple_of(slots[n] * block, block), block)
+        cols = jnp.concatenate([a_ref[:, span], b_ref[:, span], c_ref[:, span], d_ref[:, span]], axis=0)
+        rows = jnp.concatenate([grads_ref[...], next_ref[...]], axis=0)
+        out[...] = lax.dot_general(
+            cols, rows, dims, preferred_element_type=jnp.float32
+        ).astype(jnp.bfloat16)
+
+
+def grad_in_kernel(where, x_ref, own_ref, peer_ref, pull_ref, out_ref):
+    j = where[0]
+    pull = pull_ref[...]
+    for n in range(x_ref.shape[1] // (2 * LANES)):
+        cols = slice(n * LANES, (n + 1) * LANES)
+        for part, src in ((j, own_ref), (1 - j, peer_ref)):
+            span = pl.ds(pl.multiple_of((2 * n + part) * LANES, LANES), LANES)
+            wide = x_ref[:, span].astype(jnp.float32)
+            out_ref[:, span] = (src[:, cols].astype(jnp.float32) - wide * pull).astype(jnp.bfloat16)
+
+
+def last_kernel(keep_ref, first_ref, *rest):
+    others, (rows_ref, gain_ref, weight_out, gain_out) = rest[:-4], rest[-4:]
+    total = keep_ref[...].astype(jnp.float32) + first_ref[...].astype(jnp.float32)
+    for other in others:
+        total = total + other[...].astype(jnp.float32)
+    weight_out[...] = total * gain_ref[:, :1]
+    gain_sum = jnp.sum(total * rows_ref[...].astype(jnp.float32), axis=1, keepdims=True)
+    gain_out[...] = jnp.broadcast_to(gain_sum, gain_out.shape)
+
+
+def call(kernel, out_shape, scalars, arrays, hbm=0, scratch=()):
+    vmem = pl.BlockSpec(memory_space=pltpu.VMEM)
+    anywhere = pl.BlockSpec(memory_space=pl.ANY)
+    smem = pl.BlockSpec(memory_space=pltpu.SMEM)
+    many = isinstance(out_shape, (tuple, list))
+    specs = [smem] * len(scalars) + [vmem] * (len(arrays) - hbm) + [anywhere] * hbm
+    return pl.pallas_call(
+        kernel,
+        out_shape=out_shape,
+        in_specs=specs,
+        out_specs=tuple(vmem for _ in out_shape) if many else vmem,
+        scratch_shapes=scratch,
+        compiler_params=pltpu.CompilerParams(vmem_limit_bytes=48 * 1024 * 1024),
+    )(*scalars, *arrays)
+
+
+def pair_local(groups, hidden_in, norm_gain, qkv_weight, attn_cotangent):
+    depth = groups // 4
+    rows_in, cot = hidden_in[0], attn_cotangent[0]
+    tokens, width = rows_in.shape
+    block, columns = qkv_weight.shape
+    half = width // 2
+    qcols = HEADS * HD
+    i, j = lax.axis_index("inter"), lax.axis_index("intra")
+    deep, side, core = i // 4, (i // 2) % 2, i % 2
+    where = j.astype(jnp.int32)[None]
+    low, full = jnp.bfloat16, jnp.float32
+
+    def swap_pair(u):
+        return lax.ppermute(u, "intra", [(0, 1), (1, 0)])
+
+    def swap_core(u):
+        return lax.ppermute(u, "inter", [(n, n ^ 1) for n in range(groups)])
+
+    def swap_side(u):
+        return lax.ppermute(u, "inter", [(n, n ^ 2) for n in range(groups)])
+
+    def shift_deep(u, k):
+        return lax.ppermute(u, "inter", [(n, (n + 4 * k) % groups) for n in range(groups)])
+
+    def sds(shape, dtype):
+        return jax.ShapeDtypeStruct(shape, dtype)
+
+    def slot(k, l, m):
+        return (((deep - k) % depth) * 4 + (side ^ l) * 2 + (core ^ m)).astype(jnp.int32)
+
+    gain_col = norm_gain.astype(full)[:, None]
+    weight_rows = (qkv_weight.astype(full) * gain_col).astype(low)
+    by_deep = [weight_rows] + [shift_deep(weight_rows, k) for k in range(1, depth)]
+    by_side = [swap_side(u) for u in by_deep]
+    pieces, slots = [], []
+    for l, group in enumerate((by_deep, by_side)):
+        for k, u in enumerate(group):
+            pieces += [u, swap_core(u)]
+            slots += [slot(k, l, 0), slot(k, l, 1)]
+    slots = jnp.stack(slots)
+
+    x_own, x_send, half_own, half_send, rms = call(
+        split_kernel,
+        (
+            sds((tokens, half), low),
+            sds((tokens, half), low),
+            sds((tokens, half), low),
+            sds((tokens, half), low),
+            sds((tokens, LANES), full),
+        ),
+        (where,),
+        (rows_in,),
+    )
+    x_peer = swap_pair(x_send)
+    rms_peer = swap_pair(rms)
+    cot_peer = swap_pair(cot)
+    half_peer = swap_pair(half_send)
+
+    copies = [pltpu.VMEM((half, columns), low), pltpu.SemaphoreType.DMA((len(pieces),))]
+    part = call(
+        partial_kernel,
+        sds((2 * tokens, columns), low),
+        (slots,),
+        (x_own, x_peer, *pieces),
+        hbm=len(pieces),
+        scratch=copies,
+    )
+    part_peer = swap_pair(part)
+
+    local_pos = jnp.arange(tokens, dtype=jnp.int32)
+    positions = jnp.concatenate([j * tokens + local_pos, (1 - j) * tokens + local_pos])
+    cosine, sine = rope_tables(positions, HD)
+    cos_full = jnp.concatenate([cosine, cosine], axis=1)
+    sin_full = jnp.concatenate([-sine, sine], axis=1)
+
+    attn, grads, pull = call(
+        lambda *refs: attention_kernel(*refs, width=width),
+        (sds((tokens, qcols), low), sds((2 * tokens, columns), low), sds((tokens, LANES), full)),
+        (where,),
+        (part, part_peer, rms, rms_peer, cot, cot_peer, cos_full, sin_full),
+    )
+
+    grads_next = swap_core(grads)
+    own_next, peer_next = swap_core(half_own), swap_core(half_peer)
+
+    order = [k for k in range(depth) if k] + [0]
+    picks = jnp.stack(
+        [
+            ((((deep + k) % depth) * 2 + (side ^ l)) * 2 + core).astype(jnp.int32)
+            for l in (1, 0)
+            for k in order
+        ]
+    )
+    terms = call(
+        term_kernel,
+        tuple(sds((block, columns), low) for _ in range(2 * depth)),
+        (picks,),
+        (grads, grads_next, half_own, half_peer, own_next, peer_next),
+    )
+    arrived = [swap_side(u) for u in terms[:depth]]
+    kept = terms[depth:]
+    others = []
+    for n, k in enumerate(order[:-1]):
+        merged = (arrived[n].astype(full) + kept[n].astype(full)).astype(low)
+        others.append(shift_deep(merged, k))
+
+    y_own, y_send = call(
+        back_kernel,
+        (sds((tokens, half), full), sds((tokens, half), low)),
+        (slots,),
+        (grads, *pieces),
+        hbm=len(pieces),
+        scratch=copies,
+    )
+    y_peer = swap_pair(y_send)
+    grad_in = call(
+        grad_in_kernel,
+        sds((tokens, width), low),
+        (where,),
+        (rows_in, y_own, y_peer, pull),
+    )
+
+    moves = [(n, (n % groups) * 2 + n // groups) for n in range(2 * groups)]
+    rows_out = lax.ppermute(qkv_weight, ("inter", "intra"), moves)
+    gain_out = lax.ppermute(norm_gain, ("inter", "intra"), moves)
+    weight_grad, gain_wide = call(
+        last_kernel,
+        (sds((block, columns), full), sds((block, LANES), full)),
+        (),
+        (
+            kept[-1],
+            arrived[-1],
+            *others,
+            rows_out,
+            jnp.broadcast_to(gain_out.astype(full)[:, None], (block, LANES)),
+        ),
+    )
+    return (attn[None], grad_in[None], weight_grad, gain_wide[:, 0])
+
+
 def solution(mesh):
+    groups, pair = mesh.shape["inter"], mesh.shape["intra"]
+
+    def local(hidden_in, norm_gain, qkv_weight, attn_cotangent):
+        fits = pair == 2 and groups % 4 == 0 and qkv_weight.shape[0] % LANES == 0
+        args = (hidden_in, norm_gain, qkv_weight, attn_cotangent)
+        return pair_local(groups, *args) if fits else generic_local(*args)
+
     return jax.shard_map(
         local,
         mesh=mesh,

time: 227 us -> 131 us (0.58)
  blocking collectives: 122 us -> 0 us
  starting transfers between devices: 3.67 us -> 36.1 us
  Pallas kernels: 0 us -> 23.9 us
  matrix products: 18 us -> 0 us
  waiting for transfers between devices: 41.8 us -> 59.1 us
  between operations: 15.7 us -> 0.85 us
  other arithmetic: 14.6 us -> 2.52 us
  local copies, waits for them, and re-layouts: 10.3 us -> 6.43 us
    all_gather x10 -> x0, blocking collectives: 83.9 us -> none  [the longest x1 22.1 us: local(): lax.all_gather(gain_group, 'inter', axis=0, tiled=True)]
    ppermute x0 -> x33, waiting for transfers between devices: none -> 59.1 us  [the longest x8 25.9 us: swap_side(): return lax.ppermute(u, 'inter', [(n, n ^ 2) for n in range(groups)])]
    unnamed x2 -> x0, blocking collectives: 38.1 us -> none
    ppermute x0 -> x33, starting transfers between devices: none -> 36.1 us  [the longest x8 13.4 us: swap_side(): return lax.ppermute(u, 'inter', [(n, n ^ 2) for n in range(groups)])]
    reduce_scatter x1 -> x0, waiting for transfers between devices: 34 us -> none  [local(): lax.psum_scatter(term_low.astype(jnp.float32), 'inter', scatter_dimension...]
    pallas_call x0 -> x7, Pallas kernels: none -> 23.9 us  [call(): pl.pallas_call(kernel, out_shape=out_shape, in_specs=specs, out_specs=tup...]
    dot_general x9 -> x0, matrix products: 18 us -> none  [the longest x1 5.61 us: local(): jnp.einsum('tc,dc->td', grad_mixed, weight_back, preferred_element_type=j...]
    all_gather x1 -> x0, waiting for transfers between devices: 7.82 us -> none  [local(): lax.all_gather(weight_group, 'inter', axis=0, tiled=True)]
  transfers between devices with their start and end apart: 3 -> 33, of which waited for: 2 -> 12; matrix products, arithmetic and copies ran while one was open for 16% -> 1% of each run, Pallas kernels for 0% -> 16%
where the time goes in v1:
time: 131 us; the launch traced here: 129 us
  waiting for transfers between devices  59.1 us (45%)
  starting transfers between devices  36.1 us (28%)
  Pallas kernels  23.9 us (18%)
  local copies, waits for them, and re-layouts  6.43 us (5%)
  other arithmetic  2.52 us (2%)
    ppermute x8, waiting for transfers between devices, swap_side(): return lax.ppermute(u, 'inter', [(n, n ^ 2) for n in range(groups)])  25.9 us
    pallas_call x7, Pallas kernels, call(): pl.pallas_call(kernel, out_shape=out_shape, in_specs=specs, out_specs=tup...  23.9 us
    ppermute x6, waiting for transfers between devices, shift_deep(): lax.ppermute(u, 'inter', [(n, (n + 4 * k) % groups) for n in range(groups)])  21.4 us
    ppermute x8, starting transfers between devices, swap_side(): return lax.ppermute(u, 'inter', [(n, n ^ 2) for n in range(groups)])  13.4 us
    ppermute x6, starting transfers between devices, shift_deep(): lax.ppermute(u, 'inter', [(n, (n + 4 * k) % groups) for n in range(groups)])  11 us
    ppermute x6, waiting for transfers between devices, swap_pair(): return lax.ppermute(u, 'intra', [(0, 1), (1, 0)])  9.96 us
    ppermute x6, starting transfers between devices, swap_pair(): return lax.ppermute(u, 'intra', [(0, 1), (1, 0)])  9.51 us
    unnamed x28, local copies, waits for them, and re-layouts  5.56 us
  transfers between devices with their start and end apart: 33, of which 12 were waited for; matrix products, arithmetic and copies ran while one was open for 1% of the time, Pallas kernels for 16%

profile of v1, /device:TPU:0, one launch (start us, length us, event | category | flops | bytes accessed | tf_op | source)
XLA Modules:
  0.0 128.8 jit_solution(15095016647032942094)
XLA Ops:
  2.3 3.1 %collective-permute-start.2 = (bf16[128,768]{1,0:T(8,128)(2,1)S(1)}, bf16[128,768]{1,0:T(8,128)(2,1)S(1)}, u32[]{:S(2)}, u32[]{:S(2)}) collective-permute-start(bf16[128,768]{1,0:T(8,128)(2,1)S(1)} %multiply_convert_fusion.rest_0_), channel_id=1, source_target_pairs={{0,8},{2,10},{4,12},{6,14},{8,16},{10,18},{12,20},{14,22},{16,24},... | collective-permute-start | bytes 589832 | tf_op jit(solution)/shard_map/ppermute | solution.py:440
  5.4 2.6 %collective-permute-start.4 = (bf16[128,768]{1,0:T(8,128)(2,1)S(1)}, bf16[128,768]{1,0:T(8,128)(2,1)S(1)}, u32[]{:S(2)}, u32[]{:S(2)}) collective-permute-start(bf16[128,768]{1,0:T(8,128)(2,1)S(1)} %multiply_convert_fusion.rest_0_), channel_id=1, source_target_pairs={{0,16},{2,18},{4,20},{6,22},{8,24},{10,26},{12,28},{14,30},{16,0},... | collective-permute-start | bytes 589832 | tf_op jit(solution)/shard_map/ppermute | solution.py:440
  10.9 2.4 %collective-permute-done.2.rest_2_ = bf16[128,768]{1,0:T(8,128)(2,1)S(1)} collective-permute-done((bf16[128,768]{1,0:T(8,128)(2,1)S(1)}, bf16[128,768]{1,0:T(8,128)(2,1)S(1)}, u32[]{:S(2)}, u32[]{:S(2)}) %collective-permute-start.2) | collective-permute-done | bytes 196640 | tf_op jit(solution)/shard_map/ppermute | solution.py:440
  13.3 7.6 %collective-permute-done.4.rest_4_ = bf16[128,768]{1,0:T(8,128)(2,1)S(1)} collective-permute-done((bf16[128,768]{1,0:T(8,128)(2,1)S(1)}, bf16[128,768]{1,0:T(8,128)(2,1)S(1)}, u32[]{:S(2)}, u32[]{:S(2)}) %collective-permute-start.4) | collective-permute-done | bytes 196640 | tf_op jit(solution)/shard_map/ppermute | solution.py:440
  27.1 1.5 %collective-permute-start.10 = (bf16[128,768]{1,0:T(8,128)(2,1)S(1)}, bf16[128,768]{1,0:T(8,128)(2,1)S(1)}, u32[]{:S(2)}, u32[]{:S(2)}) collective-permute-start(bf16[128,768]{1,0:T(8,128)(2,1)S(1)} %collective-permute-done.2.rest_2_), channel_id=1, source_target_pairs={{0,4},{2,6},{4,0},{6,2},{8,12},{10,14},{12,8},{14,10},{16,20},{18,... | collective-permute-start | bytes 589832 | tf_op jit(solution)/shard_map/ppermute | solution.py:437
  31.3 3.6 %collective-permute-done.10.rest_10_ = bf16[128,768]{1,0:T(8,128)(2,1)S(1)} collective-permute-done((bf16[128,768]{1,0:T(8,128)(2,1)S(1)}, bf16[128,768]{1,0:T(8,128)(2,1)S(1)}, u32[]{:S(2)}, u32[]{:S(2)}) %collective-permute-start.10) | collective-permute-done | bytes 196640 | tf_op jit(solution)/shard_map/ppermute | solution.py:437
  34.9 4.2 %collective-permute-done.12.rest_12_ = bf16[128,768]{1,0:T(8,128)(2,1)S(1)} collective-permute-done((bf16[128,768]{1,0:T(8,128)(2,1)S(1)}, bf16[128,768]{1,0:T(8,128)(2,1)S(1)}, u32[]{:S(2)}, u32[]{:S(2)}) %collective-permute-start.12) | collective-permute-done | bytes 196640 | tf_op jit(solution)/shard_map/ppermute | solution.py:437
  39.1 3.4 %collective-permute-done.14.rest_14_ = bf16[128,768]{1,0:T(8,128)(2,1)S(1)} collective-permute-done((bf16[128,768]{1,0:T(8,128)(2,1)S(1)}, bf16[128,768]{1,0:T(8,128)(2,1)S(1)}, u32[]{:S(2)}, u32[]{:S(2)}) %collective-permute-start.14) | collective-permute-done | bytes 196640 | tf_op jit(solution)/shard_map/ppermute | solution.py:437
  45.7 6.9 %shard_map.76.refs_1_ = bf16[256,768]{1,0:T(8,128)(2,1)S(1)} custom-call(s32[16]{0:T(128)S(1)} %stack.94.slots, bf16[128,2048]{1,0:T(8,128)(2,1)S(1)} %copy-done.3, bf16[128,2048]{1,0:T(8,128)(2,1)} %collective-permute-done.peer_ref, bf16[128,768]{1,0:T(8,128)(2,1)S(1)} %multiply_convert_fusion.rest_0_, bf16[128,768]{1,0:T(8,128)(2,1)S(1)} %collective-permute-done.1.rest_1_, ...), custom_call_target="tpu_custom_call" | custom-call | tf_op jit(solution)/shard_map/pallas_call | solution.py:408
  55.6 8.6 %collective-permute-done.16.refs_2_ = bf16[256,768]{1,0:T(8,128)(2,1)S(1)} collective-permute-done((bf16[256,768]{1,0:T(8,128)(2,1)S(1)}, bf16[256,768]{1,0:T(8,128)(2,1)S(1)}, u32[]{:S(2)}, u32[]{:S(2)}) %collective-permute-start.16) | collective-permute-done | bytes 393248 | tf_op jit(solution)/shard_map/ppermute | solution.py:431
  64.2 2.9 %shard_map.77 = (bf16[128,512]{1,0:T(8,128)(2,1)}, bf16[256,768]{1,0:T(8,128)(2,1)S(1)}, f32[128,128]{1,0:T(8,128)S(1)}) custom-call(s32[1]{0:T(128)} %bitcast.where.refs_0_, bf16[256,768]{1,0:T(8,128)(2,1)S(1)} %shard_map.76.refs_1_, bf16[256,768]{1,0:T(8,128)(2,1)S(1)} %collective-permute-done.16.refs_2_, f32[128,128]{1,0:T(8,128)S(1)} %copy-done.11, ...), custom_call_target="tpu_custom_call" | custom-call | tf_op jit(solution)/shard_map/pallas_call | solution.py:408
  67.8 1.8 %collective-permute-done.20.next_ref = bf16[256,768]{1,0:T(8,128)(2,1)} collective-permute-done((bf16[256,768]{1,0:T(8,128)(2,1)S(1)}, bf16[256,768]{1,0:T(8,128)(2,1)}, u32[]{:S(2)}, u32[]{:S(2)}) %collective-permute-start.20) | collective-permute-done | bytes 393248 | tf_op jit(solution)/shard_map/ppermute | solution.py:434
  70.6 2.6 %shard_map.80 = (bf16[128,768]{1,0:T(8,128)(2,1)S(1)}, bf16[128,768]{1,0:T(8,128)(2,1)S(1)}, bf16[128,768]{1,0:T(8,128)(2,1)S(1)}, bf16[128,768]{1,0:T(8,128)(2,...) custom-call(s32[8]{0:T(128)S(1)} %stack.103.slots, ...), custom_call_target="tpu_custom_call" | custom-call | tf_op jit(solution)/shard_map/pallas_call | solution.py:408
  73.2 1.6 %collective-permute-start.25 = (bf16[128,768]{1,0:T(8,128)(2,1)S(1)}, bf16[128,768]{1,0:T(8,128)(2,1)S(1)}, u32[]{:S(2)}, u32[]{:S(2)}) collective-permute-start(bf16[128,768]{1,0:T(8,128)(2,1)S(1)} %get-tuple-element.36), channel_id=1, source_target_pairs={{0,4},{2,6},{4,0},{6,2},{8,12},{10,14},{12,8},{14,10},{16,20},{18,... | collective-permute-start | bytes 589832 | tf_op jit(solution)/shard_map/ppermute | solution.py:437
  76.1 7.6 %shard_map.78 = (f32[128,2048]{1,0:T(8,128)S(1)}, bf16[128,2048]{1,0:T(8,128)(2,1)S(1)}) custom-call(s32[16]{0:T(128)S(1)} %stack.94.slots, bf16[256,768]{1,0:T(8,128)(2,1)S(1)} %get-tuple-element.28.grads_ref, bf16[128,768]{1,0:T(8,128)(2,1)S(1)} %multiply_convert_fusion.rest_0_, bf16[128,768]{1,0:T(8,128)(2,1)S(1)} %collective-permute-done.1.rest_1_, ...), custom_call_target="tpu_custom_call" | custom-call | tf_op jit(solution)/shard_map/pallas_call | solution.py:408
  83.7 4.8 %collective-permute-start.19 = (bf16[128,2048]{1,0:T(8,128)(2,1)S(1)}, bf16[128,2048]{1,0:T(8,128)(2,1)S(1)}, u32[]{:S(2)}, u32[]{:S(2)}) collective-permute-start(bf16[128,2048]{1,0:T(8,128)(2,1)S(1)} %get-tuple-element.30), channel_id=1, source_target_pairs={{0,1},{1,0},{2,3},{3,2},{4,5},{5,4},{6,7},{7,6},{8,9},{9,8},{10,11... | collective-permute-start | bytes 1572872 | tf_op jit(solution)/shard_map/ppermute | solution.py:431
  88.5 4.4 %collective-permute-start.24 = (bf16[128,768]{1,0:T(8,128)(2,1)S(1)}, bf16[128,768]{1,0:T(8,128)(2,1)S(1)}, u32[]{:S(2)}, u32[]{:S(2)}) collective-permute-start(bf16[128,768]{1,0:T(8,128)(2,1)S(1)} %get-tuple-element.35), channel_id=1, source_target_pairs={{0,4},{2,6},{4,0},{6,2},{8,12},{10,14},{12,8},{14,10},{16,20},{18,... | collective-permute-start | bytes 589832 | tf_op jit(solution)/shard_map/ppermute | solution.py:437
  92.9 9.2 %collective-permute-done.27 = bf16[128,768]{1,0:T(8,128)(2,1)S(1)} collective-permute-done((bf16[128,768]{1,0:T(8,128)(2,1)S(1)}, bf16[128,768]{1,0:T(8,128)(2,1)S(1)}, u32[]{:S(2)}, u32[]{:S(2)}) %collective-permute-start.27) | collective-permute-done | bytes 196640 | tf_op jit(solution)/shard_map/ppermute | solution.py:437
  102.2 2.3 %collective-permute-start.29 = (bf16[128,768]{1,0:T(8,128)(2,1)S(1)}, bf16[128,768]{1,0:T(8,128)(2,1)S(1)}, u32[]{:S(2)}, u32[]{:S(2)}) collective-permute-start(bf16[128,768]{1,0:T(8,128)(2,1)S(1)} %get-tuple-element.40), channel_id=1, source_target_pairs={{0,4},{2,6},{4,0},{6,2},{8,12},{10,14},{12,8},{14,10},{16,20},{18,... | collective-permute-start | bytes 589832 | tf_op jit(solution)/shard_map/ppermute | solution.py:437
  104.5 5.5 %collective-permute-done.29 = bf16[128,768]{1,0:T(8,128)(2,1)S(1)} collective-permute-done((bf16[128,768]{1,0:T(8,128)(2,1)S(1)}, bf16[128,768]{1,0:T(8,128)(2,1)S(1)}, u32[]{:S(2)}, u32[]{:S(2)}) %collective-permute-start.29) | collective-permute-done | bytes 196640 | tf_op jit(solution)/shard_map/ppermute | solution.py:437
  110.0 1.5 %collective-permute-start.26 = (bf16[128,768]{1,0:T(8,128)(2,1)S(1)}, bf16[128,768]{1,0:T(8,128)(2,1)S(1)}, u32[]{:S(2)}, u32[]{:S(2)}) collective-permute-start(bf16[128,768]{1,0:T(8,128)(2,1)S(1)} %add_convert_fusion.2), channel_id=1, source_target_pairs={{0,8},{2,10},{4,12},{6,14},{8,16},{10,18},{12,20},{14,22},{16,24},... | collective-permute-start | bytes 589832 | tf_op jit(solution)/shard_map/ppermute | solution.py:440
  114.1 1.6 %shard_map.79 = bf16[128,4096]{1,0:T(8,128)(2,1)} custom-call(s32[1]{0:T(128)} %bitcast.where.refs_0_, bf16[128,4096]{1,0:T(8,128)(2,1)S(1)} %bitcast.30, f32[128,2048]{1,0:T(8,128)S(1)} %get-tuple-element.29.own_ref, bf16[128,2048]{1,0:T(8,128)(2,1)S(1)} %collective-permute-done.19.peer_ref, f32[128,128]{1,0:T(8,128)S(1)} %copy-done.9), custom_call_target="tpu_custom_call" | custom-call | tf_op jit(solution)/shard_map/pallas_call | solution.py:408
  115.7 4.0 %collective-permute-done.26.rest_0_ = bf16[128,768]{1,0:T(8,128)(2,1)S(1)} collective-permute-done((bf16[128,768]{1,0:T(8,128)(2,1)S(1)}, bf16[128,768]{1,0:T(8,128)(2,1)S(1)}, u32[]{:S(2)}, u32[]{:S(2)}) %collective-permute-start.26) | collective-permute-done | bytes 196640 | tf_op jit(solution)/shard_map/ppermute | solution.py:440
  119.7 7.4 %collective-permute-done.28.rest_1_ = bf16[128,768]{1,0:T(8,128)(2,1)S(1)} collective-permute-done((bf16[128,768]{1,0:T(8,128)(2,1)S(1)}, bf16[128,768]{1,0:T(8,128)(2,1)S(1)}, u32[]{:S(2)}, u32[]{:S(2)}) %collective-permute-start.28) | collective-permute-done | bytes 196640 | tf_op jit(solution)/shard_map/ppermute | solution.py:440
  (92 shorter events, 27.0 us)
Async XLA Ops:
  2.3 11.0 %collective-permute-start.2 = (bf16[128,768]{1,0:T(8,128)(2,1)S(1)}, bf16[128,768]{1,0:T(8,128)(2,1)S(1)}, u32[]{:S(2)}, u32[]{:S(2)}) collective-permute-start(bf16[128,768]{1,0:T(8,128)(2,1)S(1)} %multiply_convert_fusion.rest_0_), channel_id=1, source_target_pairs={{0,8},{2,10},{4,12},{6,14},{8,16},{10,18},{12,20},{14,22},{16,24},... | collective-permute-start | bytes 589832 | tf_op jit(solution)/shard_map/ppermute | solution.py:440
  5.4 15.5 %collective-permute-start.4 = (bf16[128,768]{1,0:T(8,128)(2,1)S(1)}, bf16[128,768]{1,0:T(8,128)(2,1)S(1)}, u32[]{:S(2)}, u32[]{:S(2)}) collective-permute-start(bf16[128,768]{1,0:T(8,128)(2,1)S(1)} %multiply_convert_fusion.rest_0_), channel_id=1, source_target_pairs={{0,16},{2,18},{4,20},{6,22},{8,24},{10,26},{12,28},{14,30},{16,0},... | collective-permute-start | bytes 589832 | tf_op jit(solution)/shard_map/ppermute | solution.py:440
  8.0 12.9 %collective-permute-start.6 = (bf16[128,768]{1,0:T(8,128)(2,1)S(1)}, bf16[128,768]{1,0:T(8,128)(2,1)S(1)}, u32[]{:S(2)}, u32[]{:S(2)}) collective-permute-start(bf16[128,768]{1,0:T(8,128)(2,1)S(1)} %multiply_convert_fusion.rest_0_), channel_id=1, source_target_pairs={{0,24},{2,26},{4,28},{6,30},{8,0},{10,2},{12,4},{14,6},{16,8},{18,... | collective-permute-start | bytes 589832 | tf_op jit(solution)/shard_map/ppermute | solution.py:440
  9.4 12.1 %collective-permute-start.8 = (bf16[128,768]{1,0:T(8,128)(2,1)S(1)}, bf16[128,768]{1,0:T(8,128)(2,1)S(1)}, u32[]{:S(2)}, u32[]{:S(2)}) collective-permute-start(bf16[128,768]{1,0:T(8,128)(2,1)S(1)} %multiply_convert_fusion.rest_0_), channel_id=1, source_target_pairs={{0,4},{2,6},{4,0},{6,2},{8,12},{10,14},{12,8},{14,10},{16,20},{18,... | collective-permute-start | bytes 589832 | tf_op jit(solution)/shard_map/ppermute | solution.py:437
  10.9 14.7 %collective-permute-start.1 = (bf16[128,768]{1,0:T(8,128)(2,1)S(1)}, bf16[128,768]{1,0:T(8,128)(2,1)S(1)}, u32[]{:S(2)}, u32[]{:S(2)}) collective-permute-start(bf16[128,768]{1,0:T(8,128)(2,1)S(1)} %multiply_convert_fusion.rest_0_), channel_id=1, source_target_pairs={{0,2},{2,0},{4,6},{6,4},{8,10},{10,8},{12,14},{14,12},{16,18},{18,... | collective-permute-start | bytes 589832 | tf_op jit(solution)/shard_map/ppermute | solution.py:434
  13.3 13.8 %collective-permute-start.3 = (bf16[128,768]{1,0:T(8,128)(2,1)S(1)}, bf16[128,768]{1,0:T(8,128)(2,1)S(1)}, u32[]{:S(2)}, u32[]{:S(2)}) collective-permute-start(bf16[128,768]{1,0:T(8,128)(2,1)S(1)} %collective-permute-done.2.rest_2_), channel_id=1, source_target_pairs={{0,2},{2,0},{4,6},{6,4},{8,10},{10,8},{12,14},{14,12},{16,18},{18,... | collective-permute-start | bytes 589832 | tf_op jit(solution)/shard_map/ppermute | solution.py:434
  25.6 16.9 %collective-permute-start = (bf16[128,2048]{1,0:T(8,128)(2,1)}, bf16[128,2048]{1,0:T(8,128)(2,1)}, u32[]{:S(2)}, u32[]{:S(2)}) collective-permute-start(bf16[128,2048]{1,0:T(8,128)(2,1)} %get-tuple-element.25), channel_id=1, source_target_pairs={{0,1},{1,0},{2,3},{3,2},{4,5},{5,4},{6,7},{7,6},{8,9},{9,8},{10,11... | collective-permute-start | bytes 1572872 | tf_op jit(solution)/shard_map/ppermute | solution.py:431
  28.6 10.5 %collective-permute-start.12 = (bf16[128,768]{1,0:T(8,128)(2,1)S(1)}, bf16[128,768]{1,0:T(8,128)(2,1)S(1)}, u32[]{:S(2)}, u32[]{:S(2)}) collective-permute-start(bf16[128,768]{1,0:T(8,128)(2,1)S(1)} %collective-permute-done.4.rest_4_), channel_id=1, source_target_pairs={{0,4},{2,6},{4,0},{6,2},{8,12},{10,14},{12,8},{14,10},{16,20},{18,... | collective-permute-start | bytes 589832 | tf_op jit(solution)/shard_map/ppermute | solution.py:437
  29.1 13.4 %collective-permute-start.14 = (bf16[128,768]{1,0:T(8,128)(2,1)S(1)}, bf16[128,768]{1,0:T(8,128)(2,1)S(1)}, u32[]{:S(2)}, u32[]{:S(2)}) collective-permute-start(bf16[128,768]{1,0:T(8,128)(2,1)S(1)} %collective-permute-done.6.rest_6_), channel_id=1, source_target_pairs={{0,4},{2,6},{4,0},{6,2},{8,12},{10,14},{12,8},{14,10},{16,20},{18,... | collective-permute-start | bytes 589832 | tf_op jit(solution)/shard_map/ppermute | solution.py:437
  30.6 22.6 %collective-permute-start.21 = (bf16[128,2048]{1,0:T(8,128)(2,1)}, bf16[128,2048]{1,0:T(8,128)(2,1)}, u32[]{:S(2)}, u32[]{:S(2)}) collective-permute-start(bf16[128,2048]{1,0:T(8,128)(2,1)} %get-tuple-element.33), channel_id=1, source_target_pairs={{0,1},{1,0},{2,3},{3,2},{4,5},{5,4},{6,7},{7,6},{8,9},{9,8},{10,11... | collective-permute-start | bytes 1572872 | tf_op jit(solution)/shard_map/ppermute | solution.py:431
  42.5 11.7 %collective-permute-start.17 = (f32[128,128]{1,0:T(8,128)S(1)}, f32[128,128]{1,0:T(8,128)S(1)}, u32[]{:S(2)}, u32[]{:S(2)}) collective-permute-start(f32[128,128]{1,0:T(8,128)S(1)} %get-tuple-element.26.refs_3_), channel_id=1, source_target_pairs={{0,1},{1,0},{2,3},{3,2},{4,5},{5,4},{6,7},{7,6},{8,9},{9,8},{10,11... | collective-permute-start | bytes 196616 | tf_op jit(solution)/shard_map/ppermute | solution.py:431
  43.2 12.4 %collective-permute-start.18 = (bf16[128,512]{1,0:T(8,128)(2,1)S(1)}, bf16[128,512]{1,0:T(8,128)(2,1)S(1)}, u32[]{:S(2)}, u32[]{:S(2)}) collective-permute-start(bf16[128,512]{1,0:T(8,128)(2,1)S(1)} %bitcast.31), channel_id=1, source_target_pairs={{0,1},{1,0},{2,3},{3,2},{4,5},{5,4},{6,7},{7,6},{8,9},{9,8},{10,11... | collective-permute-start | bytes 393224 | tf_op jit(solution)/shard_map/ppermute | solution.py:431
  44.6 23.2 %collective-permute-start.22 = (bf16[128,2048]{1,0:T(8,128)(2,1)}, bf16[128,2048]{1,0:T(8,128)(2,1)}, u32[]{:S(2)}, u32[]{:S(2)}) collective-permute-start(bf16[128,2048]{1,0:T(8,128)(2,1)} %copy-done.4), channel_id=1, source_target_pairs={{0,2},{2,0},{4,6},{6,4},{8,10},{10,8},{12,14},{14,12},{16,18},{18,... | collective-permute-start | bytes 1572872 | tf_op jit(solution)/shard_map/ppermute | solution.py:434
  52.6 11.6 %collective-permute-start.16 = (bf16[256,768]{1,0:T(8,128)(2,1)S(1)}, bf16[256,768]{1,0:T(8,128)(2,1)S(1)}, u32[]{:S(2)}, u32[]{:S(2)}) collective-permute-start(bf16[256,768]{1,0:T(8,128)(2,1)S(1)} %shard_map.76.refs_1_), channel_id=1, source_target_pairs={{0,1},{1,0},{2,3},{3,2},{4,5},{5,4},{6,7},{7,6},{8,9},{9,8},{10,11... | collective-permute-start | bytes 1179656 | tf_op jit(solution)/shard_map/ppermute | solution.py:431
  53.2 14.6 %collective-permute-start.23 = (bf16[128,2048]{1,0:T(8,128)(2,1)}, bf16[128,2048]{1,0:T(8,128)(2,1)}, u32[]{:S(2)}, u32[]{:S(2)}) collective-permute-start(bf16[128,2048]{1,0:T(8,128)(2,1)} %collective-permute-done.21.b_ref), channel_id=1, source_target_pairs={{0,2},{2,0},{4,6},{6,4},{8,10},{10,8},{12,14},{14,12},{16,18},{18,... | collective-permute-start | bytes 1572872 | tf_op jit(solution)/shard_map/ppermute | solution.py:434
  73.2 19.7 %collective-permute-start.25 = (bf16[128,768]{1,0:T(8,128)(2,1)S(1)}, bf16[128,768]{1,0:T(8,128)(2,1)S(1)}, u32[]{:S(2)}, u32[]{:S(2)}) collective-permute-start(bf16[128,768]{1,0:T(8,128)(2,1)S(1)} %get-tuple-element.36), channel_id=1, source_target_pairs={{0,4},{2,6},{4,0},{6,2},{8,12},{10,14},{12,8},{14,10},{16,20},{18,... | collective-permute-start | bytes 589832 | tf_op jit(solution)/shard_map/ppermute | solution.py:437
  74.8 40.9 %collective-permute-start.31 = (bf16[128,768]{1,0:T(8,128)(2,1)S(1)}, bf16[128,768]{1,0:T(8,128)(2,1)S(1)}, u32[]{:S(2)}, u32[]{:S(2)}) collective-permute-start(bf16[128,768]{1,0:T(8,128)(2,1)S(1)} %copy-done.12), channel_id=1, source_target_pairs={{0,0},{1,2},{2,4},{3,6},{4,8},{5,10},{6,12},{7,14},{8,16},{9,18},{... | collective-permute-start | bytes 589832 | tf_op jit(solution)/shard_map/ppermute | solution.py:541
  75.4 36.2 %collective-permute-start.32 = (bf16[128]{0:T(256)(128)(2,1)S(1)}, bf16[128]{0:T(256)(128)(2,1)S(1)}, u32[]{:S(2)}, u32[]{:S(2)}) collective-permute-start(bf16[128]{0:T(256)(128)(2,1)S(1)} %copy-done.13), channel_id=1, source_target_pairs={{0,0},{1,2},{2,4},{3,6},{4,8},{5,10},{6,12},{7,14},{8,16},{9,18},{... | collective-permute-start | bytes 776 | tf_op jit(solution)/shard_map/ppermute | solution.py:542
  83.7 29.1 %collective-permute-start.19 = (bf16[128,2048]{1,0:T(8,128)(2,1)S(1)}, bf16[128,2048]{1,0:T(8,128)(2,1)S(1)}, u32[]{:S(2)}, u32[]{:S(2)}) collective-permute-start(bf16[128,2048]{1,0:T(8,128)(2,1)S(1)} %get-tuple-element.30), channel_id=1, source_target_pairs={{0,1},{1,0},{2,3},{3,2},{4,5},{5,4},{6,7},{7,6},{8,9},{9,8},{10,11... | collective-permute-start | bytes 1572872 | tf_op jit(solution)/shard_map/ppermute | solution.py:431
  88.5 27.2 %collective-permute-start.24 = (bf16[128,768]{1,0:T(8,128)(2,1)S(1)}, bf16[128,768]{1,0:T(8,128)(2,1)S(1)}, u32[]{:S(2)}, u32[]{:S(2)}) collective-permute-start(bf16[128,768]{1,0:T(8,128)(2,1)S(1)} %get-tuple-element.35), channel_id=1, source_target_pairs={{0,4},{2,6},{4,0},{6,2},{8,12},{10,14},{12,8},{14,10},{16,20},{18,... | collective-permute-start | bytes 589832 | tf_op jit(solution)/shard_map/ppermute | solution.py:437
  92.9 9.3 %collective-permute-start.27 = (bf16[128,768]{1,0:T(8,128)(2,1)S(1)}, bf16[128,768]{1,0:T(8,128)(2,1)S(1)}, u32[]{:S(2)}, u32[]{:S(2)}) collective-permute-start(bf16[128,768]{1,0:T(8,128)(2,1)S(1)} %get-tuple-element.38), channel_id=1, source_target_pairs={{0,4},{2,6},{4,0},{6,2},{8,12},{10,14},{12,8},{14,10},{16,20},{18,... | collective-permute-start | bytes 589832 | tf_op jit(solution)/shard_map/ppermute | solution.py:437
  110.0 9.7 %collective-permute-start.26 = (bf16[128,768]{1,0:T(8,128)(2,1)S(1)}, bf16[128,768]{1,0:T(8,128)(2,1)S(1)}, u32[]{:S(2)}, u32[]{:S(2)}) collective-permute-start(bf16[128,768]{1,0:T(8,128)(2,1)S(1)} %add_convert_fusion.2), channel_id=1, source_target_pairs={{0,8},{2,10},{4,12},{6,14},{8,16},{10,18},{12,20},{14,22},{16,24},... | collective-permute-start | bytes 589832 | tf_op jit(solution)/shard_map/ppermute | solution.py:440
  111.6 15.5 %collective-permute-start.28 = (bf16[128,768]{1,0:T(8,128)(2,1)S(1)}, bf16[128,768]{1,0:T(8,128)(2,1)S(1)}, u32[]{:S(2)}, u32[]{:S(2)}) collective-permute-start(bf16[128,768]{1,0:T(8,128)(2,1)S(1)} %add_convert_fusion.1), channel_id=1, source_target_pairs={{0,16},{2,18},{4,20},{6,22},{8,24},{10,26},{12,28},{14,30},{16,0},... | collective-permute-start | bytes 589832 | tf_op jit(solution)/shard_map/ppermute | solution.py:440
  112.8 14.3 %collective-permute-start.30 = (bf16[128,768]{1,0:T(8,128)(2,1)S(1)}, bf16[128,768]{1,0:T(8,128)(2,1)S(1)}, u32[]{:S(2)}, u32[]{:S(2)}) collective-permute-start(bf16[128,768]{1,0:T(8,128)(2,1)S(1)} %add_convert_fusion), channel_id=1, source_target_pairs={{0,24},{2,26},{4,28},{6,30},{8,0},{10,2},{12,4},{14,6},{16,8},{18,... | collective-permute-start | bytes 589832 | tf_op jit(solution)/shard_map/ppermute | solution.py:440
  (23 other events, 152.6 us)
